TPU v7x, 256 devices: a whole 4x4x8 slice. The times are simulated.
256 devices in a mesh: dp: 64 (over y, z, core), member: 4 (over x).
Axes of the slice: x: 4, y: 4, z: 8, core: 2. Of those that a mesh axis runs over, the one named last changes fastest.
Arguments:
- features: bfloat16 [32768, 256], P('dp'), may hold values from -6 to 6
- next_features: bfloat16 [32768, 256], P('dp'), may hold values from -6 to 6
- rewards: bfloat16 [32768], P('dp'), may hold values from -6 to 6
- next_logp: bfloat16 [32768], P('dp'), may hold values from -8 to 8
- terminal: int32 [32768], P('dp'), may hold values 0 or 1
- source_ids: int32 [32768], P('dp'), may hold values from 0 to 7
- source_weight: bfloat16 [8], replicated, may hold values from 0.29882812 to 3
- subset: int32 [32768, 2], P('dp'), may hold values from 0 to 7, all different within a row
- destination: int32 [32768], P('dp'), may hold values from 0 to 63, as said below
- critic_w1: float32 [8, 2048, 256], P('member'), may hold values from -0.375 to 0.375
- critic_shift: float32 [8, 2048], P('member'), may hold values from -3 to 3
- critic_head: float32 [8, 2048], P('member'), may hold values from -0.125 to 0.125
- target_w1: bfloat16 [8, 2048, 256], P('member'), may hold values from -0.375 to 0.375
- target_mean: float32 [8, 2048], P('member'), may hold values from -2 to 2
- target_scale: float32 [8, 2048], P('member'), may hold values from 0.5 to 2
- target_shift: float32 [8, 2048], P('member'), may hold values from -3 to 3
- target_head: float32 [8, 2048], P('member'), may hold values from -0.125 to 0.125
Outputs:
- step_w1: float32 [8, 2048, 256], P('member')
- step_shift: float32 [8, 2048], P('member')
- step_head: float32 [8, 2048], P('member')
Inputs may be any that keep to these rules, and one draw needn't show every extreme that they name: `destination`: in the 512 transitions that start on one index of dp, every shard is named at least 512 // 128 times and at most 16 times, and some shard exactly 16 times. `subset`: the entries of a row differ.
All inputs are finite; a program needn't handle non-finite values. No bound on the sum of `terminal` on one device may be relied on, other than what follows from the above.
Results may differ from a plain program's by a relative error of at most 0.003.
The roundings to bfloat16 on the way count: a program that leaves them out, or rounds other values in their place, can miss the bound.
Values may be sent and summed in bfloat16 or wider, within the bound.
A program may use at most 128 MiB of HBM per device.

v0:
```python
import math
import jax
import jax.numpy as jnp
from jax import lax
from jax.sharding import PartitionSpec as P

GAMMA = 0.99
ALPHA = 0.2
EPS = 1e-05


def in_one(arrays, axis):
    ends = [0]
    for a in arrays:
        ends.append(ends[-1] + a.size)
    running = lax.psum(jnp.concatenate([a.ravel() for a in arrays]), axis)
    return tuple((running[b:e].reshape(a.shape) for a, b, e in zip(arrays, ends, ends[1:])))


def sent_to_all(array, axis):
    copies = jnp.broadcast_to(array, (lax.axis_size(axis), *array.shape))
    return lax.all_to_all(copies, axis, split_axis=0, concat_axis=0, tiled=True)


def over_copies(array, axis):
    everything = sent_to_all(array, axis)
    return jnp.sum(everything, axis=0)


def per_device(
    features,
    next_features,
    rewards,
    next_logp,
    terminal,
    source_ids,
    source_weight,
    subset,
    destination,
    critic_w1,
    critic_shift,
    critic_head,
    target_w1,
    target_mean,
    target_scale,
    target_shift,
    target_head,
):
    shards = lax.axis_size("dp")
    members = lax.axis_size("member")
    local_rows = features.shape[0]
    width = features.shape[1]
    local_critics = critic_w1.shape[0]
    total_critics = local_critics * members
    capacity = 2 * local_rows // shards
    slot_total = shards * capacity
    shard_iota = jnp.arange(shards, dtype=jnp.int32)
    picked = (destination[:, None] == shard_iota[None]).astype(jnp.int32)
    earlier = jnp.cumsum(picked, axis=0) - picked
    rank = jnp.sum(earlier * picked, axis=1)
    position = destination * capacity + rank

    def place(values):
        empty = jnp.zeros((slot_total,) + values.shape[1:], values.dtype)
        return empty.at[position].set(values).reshape((shards, capacity) + values.shape[1:])

    source_iota = jnp.arange(source_weight.shape[0], dtype=jnp.int32)
    weight_rows = jnp.sum(
        jnp.where(
            source_ids[:, None] == source_iota[None], source_weight.astype(jnp.float32)[None], 0.0
        ),
        axis=1,
    ).astype(jnp.bfloat16)
    carry_rows = (1 - terminal).astype(jnp.bfloat16)
    pre_act = jnp.einsum(
        "si,cfi->csf", next_features, target_w1, preferred_element_type=jnp.float32
    )
    active = jnp.maximum(
        (pre_act - target_mean[:, None]) * target_scale[:, None] + target_shift[:, None], 0.0
    )
    mine = jnp.sum(active * target_head[:, None], axis=2).T
    everyone = lax.all_gather(mine, "member", axis=1, tiled=True)
    critic_iota = jnp.arange(total_critics, dtype=jnp.int32)
    first = jnp.sum(jnp.where(subset[:, 0][:, None] == critic_iota[None], everyone, 0.0), axis=1)
    second = jnp.sum(jnp.where(subset[:, 1][:, None] == critic_iota[None], everyone, 0.0), axis=1)
    lowest = jnp.minimum(first, second)
    value = rewards.astype(jnp.float32) + GAMMA * carry_rows.astype(jnp.float32) * (
        lowest - ALPHA * next_logp.astype(jnp.float32)
    )
    value = value.astype(jnp.bfloat16)
    received, weight_slots, target_slots = (
        lax.all_to_all(place(features), "dp", split_axis=0, concat_axis=0, tiled=True),
        lax.all_to_all(place(weight_rows), "dp", split_axis=0, concat_axis=0, tiled=True),
        lax.all_to_all(place(value), "dp", split_axis=0, concat_axis=0, tiled=True),
    )
    rows_in = received.reshape(slot_total, width)
    weight = weight_slots.reshape(slot_total).astype(jnp.float32)
    target = target_slots.reshape(slot_total).astype(jnp.float32)
    live = (weight > 0).astype(jnp.float32)
    live_count = jnp.sum(live)
    live_col = live[:, None]

    def critic(params):
        weights, offset, output = params
        pre_act = jnp.dot(
            rows_in, weights.astype(jnp.bfloat16).T, preferred_element_type=jnp.float32
        )
        centred = pre_act - jnp.sum(pre_act * live_col, axis=0, keepdims=True) / live_count
        inverse = 1.0 / jnp.sqrt(
            jnp.sum(centred * centred * live_col, axis=0, keepdims=True) / live_count + EPS
        )
        normed = centred * inverse
        before = normed + offset[None]
        active = jnp.maximum(before, 0.0)
        value_now = jnp.sum(active * output[None], axis=1)
        slope = weight * (value_now - target)
        grad_head = jnp.dot(slope, active)
        grad_unit = jnp.where(before > 0, slope[:, None] * output[None], 0.0)
        grad_shift = jnp.sum(grad_unit, axis=0)
        unit_mean = jnp.sum(grad_unit * live_col, axis=0, keepdims=True) / live_count
        cross_mean = jnp.sum(grad_unit * normed * live_col, axis=0, keepdims=True) / live_count
        grad_pre = (inverse * (grad_unit - unit_mean - normed * cross_mean) * live_col).astype(
            jnp.bfloat16
        )
        grad_w1 = jnp.dot(grad_pre.T, rows_in, preferred_element_type=jnp.float32)
        return (grad_w1, grad_shift, grad_head)

    grad_w1, grad_shift, grad_head = lax.map(critic, (critic_w1, critic_shift, critic_head))
    hidden = critic_w1.shape[1]
    root = jnp.float32(math.sqrt(total_critics * hidden * (width + 2)))
    grad_w1, grad_shift, grad_head = in_one((grad_w1, grad_shift, grad_head), "dp")
    squares = (
        jnp.sum(grad_w1 * grad_w1)
        + jnp.sum(grad_shift * grad_shift)
        + jnp.sum(grad_head * grad_head)
    )
    norm = jnp.sqrt(over_copies(squares, "member"))
    factor = root / jnp.maximum(norm, root)
    return (grad_w1 * factor, grad_shift * factor, grad_head * factor)


def solution(mesh):
    in_specs = (
        P("dp", None),
        P("dp", None),
        P("dp"),
        P("dp"),
        P("dp"),
        P("dp"),
        P(),
        P("dp", None),
        P("dp"),
        P("member", None, None),
        P("member", None),
        P("member", None),
        P("member", None, None),
        P("member", None),
        P("member", None),
        P("member", None),
        P("member", None),
    )
    out_specs = (P("member", None, None), P("member", None), P("member", None))
    return jax.shard_map(
        per_device, mesh=mesh, in_specs=in_specs, out_specs=out_specs, check_vma=False
    )
```

profile of v0, /device:TPU:8, one launch (start us, length us, event | category | flops | bytes accessed | tf_op | source)
XLA Modules:
  0.0 378.9 jit_solution(3712643342671129567)
XLA Ops:
  8.8 4.7 %multiply_reduce_fusion.4 = f32[2,512]{1,0:T(2,128)S(1)} fusion(bf16[2,2048,256]{2,1,0:T(8,128)(2,1)S(1)} %copy-done, f32[2,2048]{1,0:T(2,128)} %param.35, f32[2,2048]{1,0:T(2,128)} %param.34, f32[2,2048]{1,0:T(2,128)} %param.33, f32[2,2048]{1,0:T(2,128)} %param.32, bf16[512,256]{1,0:T(8,128)(2,1)} %param.20), kind=kOutput, calls=%fused_computation.42 | convolution fusion | flops 1086323712 | bytes 2428928 | tf_op jit(solution)/shard_map/si,cfi->csf/dot_general | solution.py:75
  13.6 12.4 %all-gather = f32[4,2,512]{2,1,0:T(2,128)S(1)} all-gather(f32[1,2,512]{2,1,0:T(2,128)S(1)} %bitcast.140), channel_id=1, replica_groups=mesh['dp'=64,'member'=4] {'member'}, dimensions={0}, use_global_device_ids=true | all-gather | bytes 20480 | tf_op jit(solution)/shard_map/all_gather | solution.py:82
  26.0 1.2 reduce-window.6
  27.7 3.8 scatter_custom_fusion.2
  32.2 12.1 %all-to-all-start.2 = ((bf16[64,1,16]{2,1,0:T(2,128)(2,1)}), bf16[64,1,16]{2,1,0:T(2,128)(2,1)S(1)}, u32[]{:S(2)}, u32[]{:S(2)}) async-start(bf16[64,1,16]{2,1,0:T(2,128)(2,1)} %all_to_all.26), calls=%async_computation.2 | async-start | bytes 65536 | tf_op jit(solution)/shard_map/all_to_all | solution.py:94
  44.4 3.8 scatter_custom_fusion.1
  48.9 4.0 %all-to-all-done.2 = bf16[64,1,16]{2,1,0:T(2,128)(2,1)S(1)} async-done(((bf16[64,1,16]{2,1,0:T(2,128)(2,1)}), bf16[64,1,16]{2,1,0:T(2,128)(2,1)S(1)}, u32[]{:S(2)}, u32[]{:S(2)}) %all-to-all-start.2) | async-done | bytes 2080 | tf_op jit(solution)/shard_map/all_to_all | solution.py:94
  52.9 6.3 %all-to-all-start.1 = ((bf16[64,1,16]{2,1,0:T(2,128)(2,1)}), bf16[64,1,16]{2,1,0:T(2,128)(2,1)S(1)}, u32[]{:S(2)}, u32[]{:S(2)}) async-start(bf16[64,1,16]{2,1,0:T(2,128)(2,1)} %all_to_all.25), calls=%async_computation.1 | async-start | bytes 65536 | tf_op jit(solution)/shard_map/all_to_all | solution.py:93
  59.2 3.5 scatter_custom_fusion
  62.7 5.0 %all-to-all-done.1 = bf16[64,1,16]{2,1,0:T(2,128)(2,1)S(1)} async-done(((bf16[64,1,16]{2,1,0:T(2,128)(2,1)}), bf16[64,1,16]{2,1,0:T(2,128)(2,1)S(1)}, u32[]{:S(2)}, u32[]{:S(2)}) %all-to-all-start.1) | async-done | bytes 2080 | tf_op jit(solution)/shard_map/all_to_all | solution.py:93
  67.8 5.5 %all-to-all-start = ((bf16[64,16,256]{2,1,0:T(8,128)(2,1)}), bf16[64,16,256]{2,1,0:T(8,128)(2,1)S(1)}, u32[]{:S(2)}, u32[]{:S(2)}) async-start(bf16[64,16,256]{2,1,0:T(8,128)(2,1)} %bitcast.11), calls=%async_computation | async-start | bytes 1048576 | tf_op jit(solution)/shard_map/all_to_all | solution.py:92
  73.4 3.8 convert.6
  78.3 11.7 %all-to-all-done = bf16[64,16,256]{2,1,0:T(8,128)(2,1)S(1)} async-done(((bf16[64,16,256]{2,1,0:T(8,128)(2,1)}), bf16[64,16,256]{2,1,0:T(8,128)(2,1)S(1)}, u32[]{:S(2)}, u32[]{:S(2)}) %all-to-all-start) | async-done | bytes 524320 | tf_op jit(solution)/shard_map/all_to_all | solution.py:92
  90.0 50.4 %while.14 = (s32[]{:T(128)}, f32[2,2048,256]{2,1,0:T(8,128)}, f32[2,2048]{1,0:T(2,128)S(1)}, f32[2,2048]{1,0:T(2,128)S(1)}, bf16[2,2048,256]{2,1,0:T(8,128)(2,1)...) while((s32[]{:T(128)}, f32[2,2048,256]{2,1,0:T(8,128)}, ...), condition=%wide.region_18.19_spmd, body=%wide.region_11.18_spmd.sunk | while | flops 2231370752 | bytes 92651704 | solution.py:128
  90.0 2.5 multiply_reduce_fusion.12
  95.1 2.1 multiply_reduce_fusion.14
  97.2 1.4 fusion.63
  98.6 7.7 %multiply_reduce_fusion.15 = (f32[2048]{0:T(1024)S(1)}, f32[2048]{0:T(1024)S(1)}, f32[2048]{0:T(1024)S(1)}, pred[1024,2048]{1,0:T(32,128)(4,1)}) fusion(f32[1024]{0:T(1024)S(1)} %bitcast.129, f32[1024]{0:T(1024)S(1)} %subtract_multiply_fusion.4, f32[2048]{0:T(1024)S(1)} %bitcast.125, f32[2048]{0:T(1024)S(1)} %add_rsqrt_fusion.2, ...), kind=kLoop, calls=%fused_computation.12.clone.1 | loop fusion | flops 25159680 | bytes 10551296 | tf_op jit(solution)/shard_map/while/body/eval_jaxpr/reduce_sum | solution.py:120
  107.0 8.2 %fusion.62 = f32[2,2048,256]{2,1,0:T(8,128)} fusion(f32[2,2048,256]{2,1,0:T(8,128)} %get-tuple-element.217, s32[]{:T(128)S(6)} %copy.44, bf16[1024,256]{1,0:T(8,128)(2,1)S(1)} %get-tuple-element.235, pred[1024,2048]{1,0:T(32,128)(4,1)} %get-tuple-element.196, f32[2048,1024]{0,1:T(8,128)} %copy-done.1, f32[2048]{0:T(1024)S(1)} %get-tuple-element.199, ...), kind=kOutput, calls=%fused_computation.28.clone.1 | convolution fusion | flops 1094713344 | bytes 13164548 | tf_op jit(solution)/shard_map/while/body/eval_jaxpr/dot_general | solution.py:125
  115.2 2.5 multiply_reduce_fusion.12
  120.3 2.1 multiply_reduce_fusion.14
  122.4 1.4 fusion.63
  123.8 7.7 %multiply_reduce_fusion.15 = (f32[2048]{0:T(1024)S(1)}, f32[2048]{0:T(1024)S(1)}, f32[2048]{0:T(1024)S(1)}, pred[1024,2048]{1,0:T(32,128)(4,1)}) fusion(f32[1024]{0:T(1024)S(1)} %bitcast.129, f32[1024]{0:T(1024)S(1)} %subtract_multiply_fusion.4, f32[2048]{0:T(1024)S(1)} %bitcast.125, f32[2048]{0:T(1024)S(1)} %add_rsqrt_fusion.2, ...), kind=kLoop, calls=%fused_computation.12.clone.1 | loop fusion | flops 25159680 | bytes 10551296 | tf_op jit(solution)/shard_map/while/body/eval_jaxpr/reduce_sum | solution.py:120
  132.2 8.2 %fusion.62 = f32[2,2048,256]{2,1,0:T(8,128)} fusion(f32[2,2048,256]{2,1,0:T(8,128)} %get-tuple-element.217, s32[]{:T(128)S(6)} %copy.44, bf16[1024,256]{1,0:T(8,128)(2,1)S(1)} %get-tuple-element.235, pred[1024,2048]{1,0:T(32,128)(4,1)} %get-tuple-element.196, f32[2048,1024]{0,1:T(8,128)} %copy-done.1, f32[2048]{0:T(1024)S(1)} %get-tuple-element.199, ...), kind=kOutput, calls=%fused_computation.28.clone.1 | convolution fusion | flops 1094713344 | bytes 13164548 | tf_op jit(solution)/shard_map/while/body/eval_jaxpr/dot_general | solution.py:125
  140.4 4.3 %copy.33 = f32[512,2,8,128]{3,1,2,0:T(2,128)S(1)} copy(f32[512,2,8,128]{3,2,1,0:T(8,128)} %bitcast.120) | data formatting | bytes 8388608
  144.8 4.4 %pad_maximum_fusion = f32[1056768]{0:T(1024)} fusion(f32[4096]{0:T(1024)S(1)} %bitcast.133, f32[4096]{0:T(1024)S(1)} %bitcast.134, f32[1048576]{0:T(1024)S(1)} %bitcast.119), kind=kLoop, calls=%fused_computation.43 | loop fusion | flops 2113536 | bytes 8454144 | tf_op jit(solution)/shard_map/concatenate | solution.py:16
  149.2 193.5 %all-reduce.2.cloned.1.call-done = f32[1056768]{0:T(1024)} async-done(((f32[1056768]{0:T(1024)}), f32[1056768]{0:T(1024)}) %all-reduce.2.cloned.1.call-update) | async-done | bytes 4227088 | tf_op jit(solution)/shard_map/psum | solution.py:16
  342.6 3.9 %multiply_reduce_fusion.5 = f32[]{:T(128)} fusion(f32[1056768]{0:T(1024)} %all-reduce.2.cloned.1.call-done), kind=kLoop, calls=%fused_computation.44 | loop fusion | flops 2097151 | bytes 4194308 | tf_op jit(solution)/shard_map/reduce_sum | solution.py:133
  346.5 1.3 multiply_reduce_fusion.6
  349.8 9.3 %all_to_all.31 = f32[4,1,1]{2,1,0:T(1,128)S(1)} all-to-all(f32[4,1,1]{2,1,0:T(1,128)S(1)} %broadcast_in_dim.49), channel_id=1, replica_groups=mesh['dp'=64,'member'=4] {'member'}, dimensions={0} | all-to-all | bytes 32 | tf_op jit(solution)/shard_map/all_to_all | solution.py:22
  360.5 4.4 %slice_multiply_fusion = f32[1048576]{0:T(1024)} fusion(f32[1056768]{0:T(1024)} %all-reduce.2.cloned.1.call-done, f32[]{:T(128)S(6)} %div.42), kind=kLoop, calls=%fused_computation.45 | loop fusion | flops 1048576 | bytes 8388612 | tf_op jit(solution)/shard_map/mul | solution.py:139
  364.9 5.2 %mul.195 = f32[2,2048,256]{2,1,0:T(8,128)} reshape(f32[1048576]{0:T(1024)} %slice_multiply_fusion) | data formatting | bytes 8388608 | tf_op jit(solution)/shard_map/mul | solution.py:139
  (71 shorter events, 14.0 us)
Async XLA Ops:
  7.2 1.6 copy-start
  8.8 17.2 %copy-start.4 = (s32[512]{0:T(512)S(1)}, s32[512]{0:T(512)}, u32[]{:S(2)}) copy-start(s32[512]{0:T(512)} %param.27) | copy-start | bytes 6148
  8.8 18.9 %copy-start.6 = (s32[512]{0:T(512)S(1)}, s32[512]{0:T(512)}, u32[]{:S(2)}) copy-start(s32[512]{0:T(512)} %param.23) | copy-start | bytes 6148
  8.8 18.9 %copy-start.7 = (bf16[512]{0:T(512)(128)(2,1)S(1)}, bf16[512]{0:T(512)(128)(2,1)}, u32[]{:S(2)}) copy-start(bf16[512]{0:T(512)(128)(2,1)} %param.22) | copy-start | bytes 3076
  8.8 18.9 %copy-start.8 = (bf16[512]{0:T(512)(128)(2,1)S(1)}, bf16[512]{0:T(512)(128)(2,1)}, u32[]{:S(2)}) copy-start(bf16[512]{0:T(512)(128)(2,1)} %param.21) | copy-start | bytes 3076
  8.8 35.5 %copy-start.9 = (bf16[8]{0:T(256)(128)(2,1)S(1)}, bf16[8]{0:T(256)(128)(2,1)}, u32[]{:S(2)}) copy-start(bf16[8]{0:T(256)(128)(2,1)} %param.25) | copy-start | bytes 52
  8.8 35.5 %copy-start.5 = (s32[512]{0:T(512)S(1)}, s32[512]{0:T(512)}, u32[]{:S(2)}) copy-start(s32[512]{0:T(512)} %param.24) | copy-start | bytes 6148
  13.6 76.4 %copy-start.2 = (f32[2,2048]{1,0:T(2,128)S(1)}, f32[2,2048]{1,0:T(2,128)}, u32[]{:S(2)}) copy-start(f32[2,2048]{1,0:T(2,128)} %param.29) | copy-start | bytes 49156
  13.6 76.4 %copy-start.3 = (f32[2,2048]{1,0:T(2,128)S(1)}, f32[2,2048]{1,0:T(2,128)}, u32[]{:S(2)}) copy-start(f32[2,2048]{1,0:T(2,128)} %param.30) | copy-start | bytes 49156
  32.2 20.7 %all-to-all-start.2 = ((bf16[64,1,16]{2,1,0:T(2,128)(2,1)}), bf16[64,1,16]{2,1,0:T(2,128)(2,1)S(1)}, u32[]{:S(2)}, u32[]{:S(2)}) async-start(bf16[64,1,16]{2,1,0:T(2,128)(2,1)} %all_to_all.26), calls=%async_computation.2 | async-start | bytes 65536 | tf_op jit(solution)/shard_map/all_to_all | solution.py:94
  52.9 14.9 %all-to-all-start.1 = ((bf16[64,1,16]{2,1,0:T(2,128)(2,1)}), bf16[64,1,16]{2,1,0:T(2,128)(2,1)S(1)}, u32[]{:S(2)}, u32[]{:S(2)}) async-start(bf16[64,1,16]{2,1,0:T(2,128)(2,1)} %all_to_all.25), calls=%async_computation.1 | async-start | bytes 65536 | tf_op jit(solution)/shard_map/all_to_all | solution.py:93
  67.8 22.2 %all-to-all-start = ((bf16[64,16,256]{2,1,0:T(8,128)(2,1)}), bf16[64,16,256]{2,1,0:T(8,128)(2,1)S(1)}, u32[]{:S(2)}, u32[]{:S(2)}) async-start(bf16[64,16,256]{2,1,0:T(8,128)(2,1)} %bitcast.11), calls=%async_computation | async-start | bytes 1048576 | tf_op jit(solution)/shard_map/all_to_all | solution.py:92
  73.3 269.3 %all-reduce.2.cloned.1.call-start = ((), (), s32[]{:S(2)}) async-start(), calls=%async_computation.4 | async-start | bytes 8454144 | tf_op jit(solution)/shard_map/psum | solution.py:16
  92.6 4.6 %copy-start.1 = (f32[2048,1024]{0,1:T(8,128)}, f32[2048,1024]{0,1:T(8,128)S(1)}, u32[]{:S(2)}) copy-start(f32[2048,1024]{0,1:T(8,128)S(1)} %get-tuple-element.194) | copy-start | bytes 25165828 | tf_op jit(solution)/shard_map/while
  117.8 4.6 %copy-start.1 = (f32[2048,1024]{0,1:T(8,128)}, f32[2048,1024]{0,1:T(8,128)S(1)}, u32[]{:S(2)}) copy-start(f32[2048,1024]{0,1:T(8,128)S(1)} %get-tuple-element.194) | copy-start | bytes 25165828 | tf_op jit(solution)/shard_map/while
Sparse Core Ops, SparseCore 0:
  149.3 193.2 all-reduce.1
where the time goes:
time: 380 us; the launch traced here: 379 us
  waiting for transfers between devices  214 us (56%)
  other arithmetic  47.4 us (12%)
  matrix products  28.9 us (8%)
  local copies, waits for them, and re-layouts  25.7 us (7%)
  starting transfers between devices  24 us (6%)
  blocking collectives  21.7 us (6%)
  between operations  16.9 us (4%)
    psum x1, waiting for transfers between devices, in_one(): running = lax.psum(jnp.concatenate([a.ravel() for a in arrays]), axis)  193 us
    dot_general x2, matrix products, critic(): grad_w1 = jnp.dot(grad_pre.T, rows_in, preferred_element_type=jnp.float32)  16.4 us
    reduce_sum x2, other arithmetic, critic(): jnp.sum(grad_unit * live_col, axis=0, keepdims=True) / live_count  15.4 us
    all_gather x1, blocking collectives, per_device(): everyone = lax.all_gather(mine, 'member', axis=1, tiled=True)  12.4 us
    all_to_all x1, starting transfers between devices, per_device(): lax.all_to_all(place(value), 'dp', split_axis=0, concat_axis=0, tiled=True)  12.1 us
    all_to_all x1, waiting for transfers between devices, per_device(): lax.all_to_all(place(features), 'dp', split_axis=0, concat_axis=0, tiled=...  11.7 us
    scatter x3, local copies, waits for them, and re-layouts, place(): empty.at[position].set(values)  11.1 us
    all_to_all x1, blocking collectives, sent_to_all(): return lax.all_to_all(copies, axis, split_axis=0, concat_axis=0, tiled=True)  9.33 us
  transfers between devices with their start and end apart: 4, of which 4 were waited for; matrix products, arithmetic and copies ran while one was open for 3% of the time, Pallas kernels for 0%

commit v1 on v0

--- a/solution.py
+++ b/solution.py
@@ -79,7 +79,10 @@
         (pre_act - target_mean[:, None]) * target_scale[:, None] + target_shift[:, None], 0.0
     )
     mine = jnp.sum(active * target_head[:, None], axis=2).T
-    everyone = lax.all_gather(mine, "member", axis=1, tiled=True)
+    peers = lax.axis_size("member")
+    tiles = jnp.stack([mine for _ in range(peers)])
+    tiles = lax.all_to_all(tiles, "member", split_axis=0, concat_axis=0)
+    everyone = jnp.concatenate(tiles, axis=1)
     critic_iota = jnp.arange(total_critics, dtype=jnp.int32)
     first = jnp.sum(jnp.where(subset[:, 0][:, None] == critic_iota[None], everyone, 0.0), axis=1)
     second = jnp.sum(jnp.where(subset[:, 1][:, None] == critic_iota[None], everyone, 0.0), axis=1)

time: 380 us -> 374 us (0.984)
  blocking collectives: 21.7 us -> 9.33 us
  starting transfers between devices: 24 us -> 28.4 us
    all_gather x1 -> x0, blocking collectives: 12.4 us -> none  [per_device(): everyone = lax.all_gather(mine, 'member', axis=1, tiled=True)]
    all_to_all x1, starting transfers between devices: 6.34 us -> 12.1 us  [per_device(): lax.all_to_all(place(weight_rows), 'dp', split_axis=0, concat_axis=0, til...]
    all_to_all x1, starting transfers between devices: 12.1 us -> 6.4 us  [per_device(): lax.all_to_all(place(value), 'dp', split_axis=0, concat_axis=0, tiled=True)]
    all_to_all x0 -> x1, starting transfers between devices: none -> 4.3 us  [per_device(): tiles = lax.all_to_all(tiles, 'member', split_axis=0, concat_axis=0)]
  transfers between devices with their start and end apart: 4 -> 5, of which waited for: 4 -> 4; matrix products, arithmetic and copies ran while one was open for 3% -> 5% of each run, Pallas kernels for 0% -> 0%
where the time goes in v1:
time: 374 us; the launch traced here: 373 us
  waiting for transfers between devices  215 us (57%)
  other arithmetic  47.4 us (13%)
  matrix products  28.8 us (8%)
  starting transfers between devices  28.4 us (8%)
  local copies, waits for them, and re-layouts  26.2 us (7%)
  between operations  17 us (5%)
  blocking collectives  9.33 us (2%)
    psum x1, waiting for transfers between devices, in_one(): running = lax.psum(jnp.concatenate([a.ravel() for a in arrays]), axis)  195 us
    dot_general x2, matrix products, critic(): grad_w1 = jnp.dot(grad_pre.T, rows_in, preferred_element_type=jnp.float32)  16.4 us
    reduce_sum x2, other arithmetic, critic(): jnp.sum(grad_unit * live_col, axis=0, keepdims=True) / live_count  15.4 us
    all_to_all x1, starting transfers between devices, per_device(): lax.all_to_all(place(weight_rows), 'dp', split_axis=0, concat_axis=0, til...  12.1 us
    all_to_all x1, waiting for transfers between devices, per_device(): lax.all_to_all(place(features), 'dp', split_axis=0, concat_axis=0, tiled=...  11.7 us
    scatter x3, local copies, waits for them, and re-layouts, place(): empty.at[position].set(values)  11.1 us
    all_to_all x1, blocking collectives, sent_to_all(): return lax.all_to_all(copies, axis, split_axis=0, concat_axis=0, tiled=True)  9.33 us
  transfers between devices with their start and end apart: 5, of which 4 were waited for; matrix products, arithmetic and copies ran while one was open for 5% of the time, Pallas kernels for 0%

profile of v1, /device:TPU:8, one launch (start us, length us, event | category | flops | bytes accessed | tf_op | source)
XLA Modules:
  0.0 372.6 jit_solution(14756329088967809607)
XLA Ops:
  7.3 1.5 copy-done
  8.8 4.7 %multiply_reduce_fusion.4 = f32[2,512]{1,0:T(2,128)S(1)} fusion(bf16[2,2048,256]{2,1,0:T(8,128)(2,1)S(1)} %copy-done, f32[2,2048]{1,0:T(2,128)} %param.35, f32[2,2048]{1,0:T(2,128)} %param.34, f32[2,2048]{1,0:T(2,128)} %param.33, f32[2,2048]{1,0:T(2,128)} %param.32, bf16[512,256]{1,0:T(8,128)(2,1)} %param.20), kind=kOutput, calls=%fused_computation.42 | convolution fusion | flops 1086323712 | bytes 2428928 | tf_op jit(solution)/shard_map/si,cfi->csf/dot_general | solution.py:75
  14.1 4.3 %all-to-all-start.2 = ((f32[4,512,2]{1,2,0:T(2,128)}), f32[4,512,2]{1,2,0:T(2,128)S(1)}, u32[]{:S(2)}, u32[]{:S(2)}) async-start(f32[4,512,2]{1,2,0:T(2,128)} %stack.2), calls=%async_computation.2 | async-start | bytes 32768 | tf_op jit(solution)/shard_map/all_to_all | solution.py:84
  20.2 3.8 %scatter_custom_fusion.1 = bf16[1024]{0:T(1024)(128)(2,1)S(1)} fusion(s32[512]{0:T(512)S(1)} %compare_select_fusion.2, bf16[512]{0:T(512)(128)(2,1)S(1)} %select_reduce_fusion, bf16[]{:T(256)} %constant.22.clone.1), kind=kCustom, calls=%fused_computation.79 | custom fusion | bytes 2050 | tf_op jit(solution)/shard_map/scatter | solution.py:65
  24.6 12.1 %all-to-all-start.1 = ((bf16[64,1,16]{2,1,0:T(2,128)(2,1)}), bf16[64,1,16]{2,1,0:T(2,128)(2,1)S(1)}, u32[]{:S(2)}, u32[]{:S(2)}) async-start(bf16[64,1,16]{2,1,0:T(2,128)(2,1)} %all_to_all.29), calls=%async_computation.1 | async-start | bytes 65536 | tf_op jit(solution)/shard_map/all_to_all | solution.py:96
  36.9 3.8 %scatter_custom_fusion.2 = bf16[1024]{0:T(1024)(128)(2,1)S(1)} fusion(s32[512]{0:T(512)S(1)} %compare_select_fusion.2, bf16[512]{0:T(512)(128)(2,1)S(1)} %add_convert_fusion, bf16[]{:T(256)} %constant.22.clone.1), kind=kCustom, calls=%fused_computation.77 | custom fusion | bytes 2050 | tf_op jit(solution)/shard_map/scatter | solution.py:65
  41.4 3.9 %all-to-all-done.1 = bf16[64,1,16]{2,1,0:T(2,128)(2,1)S(1)} async-done(((bf16[64,1,16]{2,1,0:T(2,128)(2,1)}), bf16[64,1,16]{2,1,0:T(2,128)(2,1)S(1)}, u32[]{:S(2)}, u32[]{:S(2)}) %all-to-all-start.1) | async-done | bytes 2080 | tf_op jit(solution)/shard_map/all_to_all | solution.py:96
  45.3 6.4 %all-to-all-start.3 = ((bf16[64,1,16]{2,1,0:T(2,128)(2,1)}), bf16[64,1,16]{2,1,0:T(2,128)(2,1)S(1)}, u32[]{:S(2)}, u32[]{:S(2)}) async-start(bf16[64,1,16]{2,1,0:T(2,128)(2,1)} %all_to_all.30), calls=%async_computation.3 | async-start | bytes 65536 | tf_op jit(solution)/shard_map/all_to_all | solution.py:97
  51.7 3.5 scatter_custom_fusion
  55.2 5.1 %all-to-all-done.3 = bf16[64,1,16]{2,1,0:T(2,128)(2,1)S(1)} async-done(((bf16[64,1,16]{2,1,0:T(2,128)(2,1)}), bf16[64,1,16]{2,1,0:T(2,128)(2,1)S(1)}, u32[]{:S(2)}, u32[]{:S(2)}) %all-to-all-start.3) | async-done | bytes 2080 | tf_op jit(solution)/shard_map/all_to_all | solution.py:97
  60.3 5.5 %all-to-all-start = ((bf16[64,16,256]{2,1,0:T(8,128)(2,1)}), bf16[64,16,256]{2,1,0:T(8,128)(2,1)S(1)}, u32[]{:S(2)}, u32[]{:S(2)}) async-start(bf16[64,16,256]{2,1,0:T(8,128)(2,1)} %bitcast.11), calls=%async_computation | async-start | bytes 1048576 | tf_op jit(solution)/shard_map/all_to_all | solution.py:95
  65.9 3.8 %convert.6 = bf16[2,2048,256]{2,1,0:T(8,128)(2,1)} convert(f32[2,2048,256]{2,1,0:T(8,128)} %param.28) | non-fusion elementwise | flops 1048576 | bytes 6291456
  70.9 11.7 %all-to-all-done = bf16[64,16,256]{2,1,0:T(8,128)(2,1)S(1)} async-done(((bf16[64,16,256]{2,1,0:T(8,128)(2,1)}), bf16[64,16,256]{2,1,0:T(8,128)(2,1)S(1)}, u32[]{:S(2)}, u32[]{:S(2)}) %all-to-all-start) | async-done | bytes 524320 | tf_op jit(solution)/shard_map/all_to_all | solution.py:95
  82.5 50.4 %while.14 = (s32[]{:T(128)}, f32[2,2048,256]{2,1,0:T(8,128)}, f32[2,2048]{1,0:T(2,128)S(1)}, f32[2,2048]{1,0:T(2,128)S(1)}, bf16[2,2048,256]{2,1,0:T(8,128)(2,1)...) while((s32[]{:T(128)}, f32[2,2048,256]{2,1,0:T(8,128)}, ...), condition=%wide.region_18.19_spmd, body=%wide.region_11.18_spmd.sunk | while | flops 2231370752 | bytes 92651704 | solution.py:131
  82.6 2.5 multiply_reduce_fusion.12
  87.6 2.1 multiply_reduce_fusion.14
  89.7 1.4 fusion.63
  91.2 7.7 %multiply_reduce_fusion.15 = (f32[2048]{0:T(1024)S(1)}, f32[2048]{0:T(1024)S(1)}, f32[2048]{0:T(1024)S(1)}, pred[1024,2048]{1,0:T(32,128)(4,1)}) fusion(f32[1024]{0:T(1024)S(1)} %bitcast.125, f32[1024]{0:T(1024)S(1)} %subtract_multiply_fusion.4, f32[2048]{0:T(1024)S(1)} %bitcast.121, f32[2048]{0:T(1024)S(1)} %add_rsqrt_fusion.2, ...), kind=kLoop, calls=%fused_computation.12.clone.1 | loop fusion | flops 25159680 | bytes 10551296 | tf_op jit(solution)/shard_map/while/body/eval_jaxpr/reduce_sum | solution.py:123
  99.6 8.2 %fusion.62 = f32[2,2048,256]{2,1,0:T(8,128)} fusion(f32[2,2048,256]{2,1,0:T(8,128)} %get-tuple-element.217, s32[]{:T(128)S(6)} %copy.44, bf16[1024,256]{1,0:T(8,128)(2,1)S(1)} %get-tuple-element.235, pred[1024,2048]{1,0:T(32,128)(4,1)} %get-tuple-element.196, f32[2048,1024]{0,1:T(8,128)} %copy-done.1, f32[2048]{0:T(1024)S(1)} %get-tuple-element.199, ...), kind=kOutput, calls=%fused_computation.28.clone.1 | convolution fusion | flops 1094713344 | bytes 13164548 | tf_op jit(solution)/shard_map/while/body/eval_jaxpr/dot_general | solution.py:128
  107.8 2.5 multiply_reduce_fusion.12
  112.9 2.1 multiply_reduce_fusion.14
  114.9 1.4 fusion.63
  116.4 7.7 %multiply_reduce_fusion.15 = (f32[2048]{0:T(1024)S(1)}, f32[2048]{0:T(1024)S(1)}, f32[2048]{0:T(1024)S(1)}, pred[1024,2048]{1,0:T(32,128)(4,1)}) fusion(f32[1024]{0:T(1024)S(1)} %bitcast.125, f32[1024]{0:T(1024)S(1)} %subtract_multiply_fusion.4, f32[2048]{0:T(1024)S(1)} %bitcast.121, f32[2048]{0:T(1024)S(1)} %add_rsqrt_fusion.2, ...), kind=kLoop, calls=%fused_computation.12.clone.1 | loop fusion | flops 25159680 | bytes 10551296 | tf_op jit(solution)/shard_map/while/body/eval_jaxpr/reduce_sum | solution.py:123
  124.8 8.2 %fusion.62 = f32[2,2048,256]{2,1,0:T(8,128)} fusion(f32[2,2048,256]{2,1,0:T(8,128)} %get-tuple-element.217, s32[]{:T(128)S(6)} %copy.44, bf16[1024,256]{1,0:T(8,128)(2,1)S(1)} %get-tuple-element.235, pred[1024,2048]{1,0:T(32,128)(4,1)} %get-tuple-element.196, f32[2048,1024]{0,1:T(8,128)} %copy-done.1, f32[2048]{0:T(1024)S(1)} %get-tuple-element.199, ...), kind=kOutput, calls=%fused_computation.28.clone.1 | convolution fusion | flops 1094713344 | bytes 13164548 | tf_op jit(solution)/shard_map/while/body/eval_jaxpr/dot_general | solution.py:128
  133.0 4.3 %copy.33 = f32[512,2,8,128]{3,1,2,0:T(2,128)S(1)} copy(f32[512,2,8,128]{3,2,1,0:T(8,128)} %bitcast.116) | data formatting | bytes 8388608
  137.3 4.4 %pad_maximum_fusion = f32[1056768]{0:T(1024)} fusion(f32[4096]{0:T(1024)S(1)} %bitcast.129, f32[4096]{0:T(1024)S(1)} %bitcast.130, f32[1048576]{0:T(1024)S(1)} %bitcast.115), kind=kLoop, calls=%fused_computation.43 | loop fusion | flops 2113536 | bytes 8454144 | tf_op jit(solution)/shard_map/concatenate | solution.py:16
  141.7 194.6 %all-reduce.2.cloned.1.call-done = f32[1056768]{0:T(1024)} async-done(((f32[1056768]{0:T(1024)}), f32[1056768]{0:T(1024)}) %all-reduce.2.cloned.1.call-update) | async-done | bytes 4227088 | tf_op jit(solution)/shard_map/psum | solution.py:16
  336.3 3.9 %multiply_reduce_fusion.5 = f32[]{:T(128)} fusion(f32[1056768]{0:T(1024)} %all-reduce.2.cloned.1.call-done), kind=kLoop, calls=%fused_computation.44 | loop fusion | flops 2097151 | bytes 4194308 | tf_op jit(solution)/shard_map/reduce_sum | solution.py:136
  340.2 1.3 multiply_reduce_fusion.6
  343.5 9.3 %all_to_all.36 = f32[4,1,1]{2,1,0:T(1,128)S(1)} all-to-all(f32[4,1,1]{2,1,0:T(1,128)S(1)} %broadcast_in_dim.70), channel_id=1, replica_groups=mesh['dp'=64,'member'=4] {'member'}, dimensions={0} | all-to-all | bytes 32 | tf_op jit(solution)/shard_map/all_to_all | solution.py:22
  354.2 4.4 %slice_multiply_fusion = f32[1048576]{0:T(1024)} fusion(f32[1056768]{0:T(1024)} %all-reduce.2.cloned.1.call-done, f32[]{:T(128)S(6)} %div.42), kind=kLoop, calls=%fused_computation.45 | loop fusion | flops 1048576 | bytes 8388612 | tf_op jit(solution)/shard_map/mul | solution.py:142
  358.6 5.2 %mul.195 = f32[2,2048,256]{2,1,0:T(8,128)} reshape(f32[1048576]{0:T(1024)} %slice_multiply_fusion) | data formatting | bytes 8388608 | tf_op jit(solution)/shard_map/mul | solution.py:142
  (75 shorter events, 14.3 us)
Async XLA Ops:
  7.2 1.6 copy-start
  7.2 11.2 %copy-start.10 = (bf16[8]{0:T(256)(128)(2,1)S(1)}, bf16[8]{0:T(256)(128)(2,1)}, u32[]{:S(2)}) copy-start(bf16[8]{0:T(256)(128)(2,1)} %param.25) | copy-start | bytes 52
  7.2 11.2 %copy-start.5 = (s32[512,2]{0,1:T(2,128)S(1)}, s32[512,2]{0,1:T(2,128)}, u32[]{:S(2)}) copy-start(s32[512,2]{0,1:T(2,128)} %param.26) | copy-start | bytes 12292
  7.2 11.2 %copy-start.4 = (s32[512]{0:T(512)S(1)}, s32[512]{0:T(512)}, u32[]{:S(2)}) copy-start(s32[512]{0:T(512)} %param.27) | copy-start | bytes 6148
  7.2 12.9 %copy-start.6 = (s32[512]{0:T(512)S(1)}, s32[512]{0:T(512)}, u32[]{:S(2)}) copy-start(s32[512]{0:T(512)} %param.24) | copy-start | bytes 6148
  7.2 29.6 %copy-start.7 = (s32[512]{0:T(512)S(1)}, s32[512]{0:T(512)}, u32[]{:S(2)}) copy-start(s32[512]{0:T(512)} %param.23) | copy-start | bytes 6148
  7.2 29.6 %copy-start.8 = (bf16[512]{0:T(512)(128)(2,1)S(1)}, bf16[512]{0:T(512)(128)(2,1)}, u32[]{:S(2)}) copy-start(bf16[512]{0:T(512)(128)(2,1)} %param.22) | copy-start | bytes 3076
  7.2 29.6 %copy-start.9 = (bf16[512]{0:T(512)(128)(2,1)S(1)}, bf16[512]{0:T(512)(128)(2,1)}, u32[]{:S(2)}) copy-start(bf16[512]{0:T(512)(128)(2,1)} %param.21) | copy-start | bytes 3076
  13.5 69.1 %copy-start.2 = (f32[2,2048]{1,0:T(2,128)S(1)}, f32[2,2048]{1,0:T(2,128)}, u32[]{:S(2)}) copy-start(f32[2,2048]{1,0:T(2,128)} %param.29) | copy-start | bytes 49156
  13.5 69.1 %copy-start.3 = (f32[2,2048]{1,0:T(2,128)S(1)}, f32[2,2048]{1,0:T(2,128)}, u32[]{:S(2)}) copy-start(f32[2,2048]{1,0:T(2,128)} %param.30) | copy-start | bytes 49156
  14.1 10.6 %all-to-all-start.2 = ((f32[4,512,2]{1,2,0:T(2,128)}), f32[4,512,2]{1,2,0:T(2,128)S(1)}, u32[]{:S(2)}, u32[]{:S(2)}) async-start(f32[4,512,2]{1,2,0:T(2,128)} %stack.2), calls=%async_computation.2 | async-start | bytes 32768 | tf_op jit(solution)/shard_map/all_to_all | solution.py:84
  24.6 20.7 %all-to-all-start.1 = ((bf16[64,1,16]{2,1,0:T(2,128)(2,1)}), bf16[64,1,16]{2,1,0:T(2,128)(2,1)S(1)}, u32[]{:S(2)}, u32[]{:S(2)}) async-start(bf16[64,1,16]{2,1,0:T(2,128)(2,1)} %all_to_all.29), calls=%async_computation.1 | async-start | bytes 65536 | tf_op jit(solution)/shard_map/all_to_all | solution.py:96
  45.3 15.0 %all-to-all-start.3 = ((bf16[64,1,16]{2,1,0:T(2,128)(2,1)}), bf16[64,1,16]{2,1,0:T(2,128)(2,1)S(1)}, u32[]{:S(2)}, u32[]{:S(2)}) async-start(bf16[64,1,16]{2,1,0:T(2,128)(2,1)} %all_to_all.30), calls=%async_computation.3 | async-start | bytes 65536 | tf_op jit(solution)/shard_map/all_to_all | solution.py:97
  60.3 22.2 %all-to-all-start = ((bf16[64,16,256]{2,1,0:T(8,128)(2,1)}), bf16[64,16,256]{2,1,0:T(8,128)(2,1)S(1)}, u32[]{:S(2)}, u32[]{:S(2)}) async-start(bf16[64,16,256]{2,1,0:T(8,128)(2,1)} %bitcast.11), calls=%async_computation | async-start | bytes 1048576 | tf_op jit(solution)/shard_map/all_to_all | solution.py:95
  65.8 270.5 %all-reduce.2.cloned.1.call-start = ((), (), s32[]{:S(2)}) async-start(), calls=%async_computation.5 | async-start | bytes 8454144 | tf_op jit(solution)/shard_map/psum | solution.py:16
  85.1 4.6 %copy-start.1 = (f32[2048,1024]{0,1:T(8,128)}, f32[2048,1024]{0,1:T(8,128)S(1)}, u32[]{:S(2)}) copy-start(f32[2048,1024]{0,1:T(8,128)S(1)} %get-tuple-element.194) | copy-start | bytes 25165828 | tf_op jit(solution)/shard_map/while
  110.3 4.6 %copy-start.1 = (f32[2048,1024]{0,1:T(8,128)}, f32[2048,1024]{0,1:T(8,128)S(1)}, u32[]{:S(2)}) copy-start(f32[2048,1024]{0,1:T(8,128)S(1)} %get-tuple-element.194) | copy-start | bytes 25165828 | tf_op jit(solution)/shard_map/while
Sparse Core Ops, SparseCore 0:
  141.8 194.4 all-reduce.1
